TPU v7x, 32 devices: a whole 2x2x4 slice. The times are simulated.
32 devices in a mesh: section: 8 (over z, x), dp: 4 (over y, core).
Axes of the slice: x: 2, y: 2, z: 4, core: 2. Of those that a mesh axis runs over, the one named last changes fastest.
Arguments:
- carry_act: bfloat16 [8, 32, 2304], P('section', 'dp'), may hold values from -6 to 6
- carry_act_tan: bfloat16 [8, 32, 2304], P('section', 'dp'), may hold values from -6 to 6
- carry_adj: bfloat16 [8, 32, 2304], P('section', 'dp'), may hold values from -0.75 to 0.75
- carry_adj_tan: bfloat16 [8, 32, 2304], P('section', 'dp'), may hold values from -0.75 to 0.75
- fresh_act: bfloat16 [2, 32, 2304], P(None, 'dp'), may hold values from -6 to 6
- loss_cot: bfloat16 [2, 32, 2304], P(None, 'dp'), may hold values from -0.75 to 0.75
- stash_act: bfloat16 [8, 2, 32, 2304], P('section', None, 'dp'), may hold values from -6 to 6
- stash_act_tan: bfloat16 [8, 2, 32, 2304], P('section', None, 'dp'), may hold values from -6 to 6
- norm_gain: bfloat16 [8, 2304], P('section'), may hold values from 0.25 to 1.75
- up_weight: bfloat16 [8, 2304, 4608], P('section', None, 'dp'), may hold values from -0.125 to 0.125
- down_weight: bfloat16 [8, 4608, 2304], P('section', 'dp'), may hold values from -0.09375 to 0.09375
- up_dir: bfloat16 [8, 2304, 4608], P('section', None, 'dp'), may hold values from -0.125 to 0.125
- down_dir: bfloat16 [8, 4608, 2304], P('section', 'dp'), may hold values from -0.09375 to 0.09375
Outputs:
- next_act: bfloat16 [8, 32, 2304], P('section', 'dp')
- next_act_tan: bfloat16 [8, 32, 2304], P('section', 'dp')
- next_adj: bfloat16 [8, 32, 2304], P('section', 'dp')
- next_adj_tan: bfloat16 [8, 32, 2304], P('section', 'dp')
- hvp_up: bfloat16 [8, 2304, 4608], P('section', None, 'dp')
- hvp_down: bfloat16 [8, 4608, 2304], P('section', 'dp')
All inputs are finite; a program needn't handle non-finite values.
Results may differ from a plain program's by a relative error of at most 0.02.
Values may be sent and summed in bfloat16 or wider, within the bound.
A program may use at most 128 MiB of HBM per device.

v0:
```python
import jax
import jax.numpy as jnp
from jax import lax
from jax.sharding import PartitionSpec as P

TICKS = 2


sqrt_two_over_pi = 0.7978845608028654
cubic_coef = 0.044715
norm_eps = 1e-06


def passed_along(value, axis, steps):
    count = lax.axis_size(axis)
    leading, last = (max(0, -steps), min(count, count - steps))
    return lax.ppermute(value, axis, [(source, source + steps) for source in range(leading, last)])


def gelu_parts(linear):
    inner_arg = sqrt_two_over_pi * (linear + cubic_coef * linear * linear * linear)
    first_slope = sqrt_two_over_pi * (1.0 + 3.0 * cubic_coef * linear * linear)
    second_slope = 6.0 * sqrt_two_over_pi * cubic_coef * linear
    tanh_value = jnp.tanh(inner_arg)
    sech_square = 1.0 - tanh_value * tanh_value
    gelu_value = 0.5 * linear * (1.0 + tanh_value)
    gelu_first = 0.5 * (1.0 + tanh_value) + 0.5 * linear * sech_square * first_slope
    gelu_second = sech_square * (
        first_slope - linear * tanh_value * first_slope * first_slope + 0.5 * linear * second_slope
    )
    return (gelu_value, gelu_first, gelu_second)


def matrix_product(left, right):
    return jnp.dot(left, right, preferred_element_type=jnp.float32)


def product_last(left, right):
    return lax.dot_general(
        left, right, (((1,), (1,)), ((), ())), preferred_element_type=jnp.float32
    )


def product_first(left, right):
    return lax.dot_general(
        left, right, (((0,), (0,)), ((), ())), preferred_element_type=jnp.float32
    )


def norm_stats(rows, rows_tan):
    values = rows.astype(jnp.float32)
    values_tan = rows_tan.astype(jnp.float32)
    inverse = lax.rsqrt(jnp.mean(values * values, axis=-1, keepdims=True) + norm_eps)
    inverse_tan = -(inverse * inverse * inverse) * jnp.mean(
        values * values_tan, axis=-1, keepdims=True
    )
    return (values, values_tan, inverse, inverse_tan)


def norm_rows(rows, rows_tan, gain_row):
    values, values_tan, inverse, inverse_tan = norm_stats(rows, rows_tan)
    gain_wide = gain_row.astype(jnp.float32)
    normed = (values * inverse * gain_wide).astype(jnp.bfloat16)
    normed_tan = ((values_tan * inverse + values * inverse_tan) * gain_wide).astype(jnp.bfloat16)
    return (normed, normed_tan)


def norm_back(rows, rows_tan, gain_row, arriving, arriving_tan, summed, summed_tan):
    values, values_tan, inverse, inverse_tan = norm_stats(rows, rows_tan)
    gain_wide = gain_row.astype(jnp.float32)
    weighted = summed * gain_wide
    weighted_tan = summed_tan * gain_wide
    moment = jnp.mean(values * weighted, axis=-1, keepdims=True)
    moment_tan = jnp.mean(values_tan * weighted + values * weighted_tan, axis=-1, keepdims=True)
    inverse_cube = inverse * inverse * inverse
    returned = arriving.astype(jnp.float32) + inverse * weighted - inverse_cube * values * moment
    returned_tan = (
        arriving_tan.astype(jnp.float32)
        + inverse_tan * weighted
        + inverse * weighted_tan
        - 3.0 * inverse * inverse * inverse_tan * values * moment
        - inverse_cube * values_tan * moment
        - inverse_cube * values * moment_tan
    )
    return (returned.astype(jnp.bfloat16), returned_tan.astype(jnp.bfloat16))


def branch_forward(normed, normed_tan, up_local, down_local, up_direction, down_direction):
    linear = matrix_product(normed, up_local)
    linear_tan = matrix_product(normed_tan, up_local) + matrix_product(normed, up_direction)
    gelu_value, gelu_first, gelu_second = gelu_parts(linear)
    hidden = gelu_value.astype(jnp.bfloat16)
    hidden_tan = (gelu_first * linear_tan).astype(jnp.bfloat16)
    partial_value = matrix_product(hidden, down_local)
    partial_tan = matrix_product(hidden_tan, down_local) + matrix_product(hidden, down_direction)
    return (partial_value, partial_tan)


def branch_backward(
    stash_normed,
    stash_normed_tan,
    adjoint_all,
    adjoint_all_tan,
    up_local,
    down_local,
    up_direction,
    down_direction,
):
    linear = matrix_product(stash_normed, up_local)
    linear_tan = matrix_product(stash_normed_tan, up_local) + matrix_product(
        stash_normed, up_direction
    )
    gelu_value, gelu_first, gelu_second = gelu_parts(linear)
    hidden = gelu_value.astype(jnp.bfloat16)
    hidden_tan = (gelu_first * linear_tan).astype(jnp.bfloat16)
    upstream = product_last(adjoint_all, down_local)
    upstream_tan = product_last(adjoint_all_tan, down_local) + product_last(
        adjoint_all, down_direction
    )
    deltas = (upstream * gelu_first).astype(jnp.bfloat16)
    deltas_tan = (upstream_tan * gelu_first + upstream * gelu_second * linear_tan).astype(
        jnp.bfloat16
    )
    curvature_down = product_first(hidden_tan, adjoint_all) + product_first(hidden, adjoint_all_tan)
    curvature_up = product_first(stash_normed_tan, deltas) + product_first(stash_normed, deltas_tan)
    partial_value = product_last(deltas, up_local)
    partial_tan = product_last(deltas_tan, up_local) + product_last(deltas, up_direction)
    return (partial_value, partial_tan, curvature_up, curvature_down)


def gather_rows(lead_rows, lead_tan, stash_rows, stash_tan, adjoint_rows, adjoint_tan):
    forward_rows = (
        lax.all_gather(lead_rows, "dp", axis=0, tiled=True),
        lax.all_gather(lead_tan, "dp", axis=0, tiled=True),
    )
    backward_rows = (
        lax.all_gather(stash_rows, "dp", axis=0, tiled=True),
        lax.all_gather(stash_tan, "dp", axis=0, tiled=True),
        lax.all_gather(adjoint_rows, "dp", axis=0, tiled=True),
        lax.all_gather(adjoint_tan, "dp", axis=0, tiled=True),
    )
    return (forward_rows, backward_rows)


def reduce_rows(forward_term, forward_tan, backward_term, backward_tan):
    summed_forward = (
        lax.psum_scatter(
            forward_term.astype(jnp.bfloat16), "dp", scatter_dimension=0, tiled=True
        ).astype(jnp.float32),
        lax.psum_scatter(
            forward_tan.astype(jnp.bfloat16), "dp", scatter_dimension=0, tiled=True
        ).astype(jnp.float32),
    )
    summed_backward = (
        lax.psum_scatter(
            backward_term.astype(jnp.bfloat16), "dp", scatter_dimension=0, tiled=True
        ).astype(jnp.float32),
        lax.psum_scatter(
            backward_tan.astype(jnp.bfloat16), "dp", scatter_dimension=0, tiled=True
        ).astype(jnp.float32),
    )
    return (summed_forward, summed_backward)


def shards(
    carry_act,
    carry_act_tan,
    carry_adj,
    carry_adj_tan,
    fresh_act,
    loss_cot,
    stash_act,
    stash_act_tan,
    norm_gain,
    up_weight,
    down_weight,
    up_dir,
    down_dir,
):
    section_index = lax.axis_index("section")
    section_count = lax.axis_size("section")
    at_first = section_index == 0
    at_last = section_index == section_count - 1
    gain_row = norm_gain[0]
    up_local = up_weight[0]
    down_local = down_weight[0]
    up_direction = up_dir[0]
    down_direction = down_dir[0]
    activation, activation_tan = (carry_act[0], carry_act_tan[0])
    adjoint, adjoint_tan = (carry_adj[0], carry_adj_tan[0])
    total_up = jnp.zeros(up_local.shape, jnp.float32)
    total_down = jnp.zeros(down_local.shape, jnp.float32)
    for tick_index in range(TICKS):
        fresh_rows = fresh_act[tick_index]
        cotangent = loss_cot[tick_index]
        zero_rows = jnp.zeros_like(fresh_rows)
        stash_rows = stash_act[0, tick_index]
        stash_tan = stash_act_tan[0, tick_index]
        moved_forward = passed_along((activation, activation_tan), "section", 1)
        moved_backward = passed_along((adjoint, adjoint_tan), "section", -1)
        input_rows = jnp.where(at_first, fresh_rows, moved_forward[0])
        input_tan = jnp.where(at_first, zero_rows, moved_forward[1])
        arriving = jnp.where(at_last, cotangent, moved_backward[0])
        arriving_tan = jnp.where(at_last, zero_rows, moved_backward[1])
        normed, normed_tan = norm_rows(input_rows, input_tan, gain_row)
        stash_normed, stash_normed_tan = norm_rows(stash_rows, stash_tan, gain_row)
        forward_rows, backward_rows = gather_rows(
            normed, normed_tan, stash_normed, stash_normed_tan, arriving, arriving_tan
        )
        normed_all, normed_all_tan = (forward_rows[0], forward_rows[1])
        stash_all, stash_all_tan = (backward_rows[0], backward_rows[1])
        adjoint_all, adjoint_all_tan = (backward_rows[2], backward_rows[3])
        partial_value, partial_tan = branch_forward(
            normed_all, normed_all_tan, up_local, down_local, up_direction, down_direction
        )
        back_partial, back_partial_tan, curvature_up, curvature_down = branch_backward(
            stash_all,
            stash_all_tan,
            adjoint_all,
            adjoint_all_tan,
            up_local,
            down_local,
            up_direction,
            down_direction,
        )
        summed_forward, summed_backward = reduce_rows(
            partial_value, partial_tan, back_partial, back_partial_tan
        )
        total_up = total_up + curvature_up
        total_down = total_down + curvature_down
        activation = (input_rows.astype(jnp.float32) + summed_forward[0]).astype(jnp.bfloat16)
        activation_tan = (input_tan.astype(jnp.float32) + summed_forward[1]).astype(jnp.bfloat16)
        adjoint, adjoint_tan = norm_back(
            stash_rows,
            stash_tan,
            gain_row,
            arriving,
            arriving_tan,
            summed_backward[0],
            summed_backward[1],
        )
    return (
        activation[None],
        activation_tan[None],
        adjoint[None],
        adjoint_tan[None],
        total_up.astype(jnp.bfloat16)[None],
        total_down.astype(jnp.bfloat16)[None],
    )


def solution(mesh):
    in_specs = (
        P("section", "dp", None),
        P("section", "dp", None),
        P("section", "dp", None),
        P("section", "dp", None),
        P(None, "dp", None),
        P(None, "dp", None),
        P("section", None, "dp", None),
        P("section", None, "dp", None),
        P("section", None),
        P("section", None, "dp"),
        P("section", "dp", None),
        P("section", None, "dp"),
        P("section", "dp", None),
    )
    out_specs = (
        P("section", "dp", None),
        P("section", "dp", None),
        P("section", "dp", None),
        P("section", "dp", None),
        P("section", None, "dp"),
        P("section", "dp", None),
    )
    return jax.shard_map(shards, mesh=mesh, in_specs=in_specs, out_specs=out_specs, check_vma=False)
```

profile of v0, /device:TPU:0, one launch (start us, length us, event | category | flops | bytes accessed | tf_op | source)
XLA Modules:
  0.0 396.7 jit_solution(5366362785262543976)
XLA Ops:
  10.1 6.3 %collective-permute-start.2 = (bf16[8,2304]{1,0:T(8,128)(2,1)}, bf16[8,2304]{1,0:T(8,128)(2,1)S(1)}, u32[]{:S(2)}, u32[]{:S(2)}) collective-permute-start(bf16[8,2304]{1,0:T(8,128)(2,1)} %bitcast.246), channel_id=1, source_target_pairs={{0,4},{4,8},{8,12},{12,16},{16,20},{20,24},{24,28},{1,5},{5,9},{9,... | collective-permute-start | bytes 110600 | tf_op jit(solution)/shard_map/ppermute | solution.py:17
  23.8 5.5 %all_gather.41 = bf16[32,2304]{1,0:T(8,128)(2,1)S(1)} all-gather(bf16[8,2304]{1,0:T(8,128)(2,1)S(1)} %get-tuple-element.31), channel_id=1, replica_groups=mesh['section'=8,'dp'=4] {'dp'}, dimensions={0}, use_global_device_ids=true | all-gather | bytes 184320 | tf_op jit(solution)/shard_map/all_gather | solution.py:137
  29.3 5.6 %all_gather.45 = bf16[32,2304]{1,0:T(8,128)(2,1)S(1)} all-gather(bf16[8,2304]{1,0:T(8,128)(2,1)S(1)} %get-tuple-element.30), channel_id=1, replica_groups=mesh['section'=8,'dp'=4] {'dp'}, dimensions={0}, use_global_device_ids=true | all-gather | bytes 184320 | tf_op jit(solution)/shard_map/all_gather | solution.py:138
  54.4 5.6 %fusion.304 = f32[2304,1152]{1,0:T(8,128)} fusion(bf16[32,2304]{1,0:T(8,128)(2,1)S(1)} %all_gather.45, bf16[32,1152]{1,0:T(8,128)(2,1)S(1)} %get-tuple-element.48), kind=kOutput, calls=%fused_computation.331 | convolution fusion | flops 169869312 | bytes 10838016 | tf_op jit(solution)/shard_map/dot_general | solution.py:45
  61.6 5.6 %all_gather.44 = bf16[32,2304]{1,0:T(8,128)(2,1)S(1)} all-gather(bf16[8,2304]{1,0:T(8,128)(2,1)S(1)} %broadcast_select_fusion.1), channel_id=1, replica_groups=mesh['section'=8,'dp'=4] {'dp'}, dimensions={0}, use_global_device_ids=true | all-gather | bytes 184320 | tf_op jit(solution)/shard_map/all_gather | solution.py:140
  67.2 5.5 %fusion.242 = f32[1152,2304]{1,0:T(8,128)} fusion(bf16[32,2304]{1,0:T(8,128)(2,1)S(1)} %all_gather.44, f32[32,1152]{1,0:T(8,128)S(1)} %fusion.56), kind=kOutput, calls=%fused_computation.240 | convolution fusion | flops 170201088 | bytes 10911744 | tf_op jit(solution)/shard_map/dot_general | solution.py:45
  81.8 15.2 %reduce-scatter.21.cloned.1.call-done = bf16[8,2304]{1,0:T(8,128)(2,1)} async-done(((bf16[32,2304]{1,0:T(8,128)(2,1)}), bf16[8,2304]{1,0:T(8,128)(2,1)}) %reduce-scatter.21.cloned.1.call-update) | async-done | bytes 36880 | tf_op jit(solution)/shard_map/reduce_scatter | solution.py:158
  97.0 22.7 %reduce-scatter.17.cloned.1.call-done = bf16[8,2304]{1,0:T(8,128)(2,1)} async-done(((bf16[32,2304]{1,0:T(8,128)(2,1)}), bf16[8,2304]{1,0:T(8,128)(2,1)}) %reduce-scatter.17.cloned.1.call-update) | async-done | bytes 36880 | tf_op jit(solution)/shard_map/reduce_scatter | solution.py:155
  121.7 16.8 %all_gather.43 = bf16[32,2304]{1,0:T(8,128)(2,1)S(1)} all-gather(bf16[8,2304]{1,0:T(8,128)(2,1)S(1)} %get-tuple-element.29), channel_id=1, replica_groups=mesh['section'=8,'dp'=4] {'dp'}, dimensions={0}, use_global_device_ids=true | all-gather | bytes 184320 | tf_op jit(solution)/shard_map/all_gather | solution.py:137
  147.4 5.6 %all_gather.47 = bf16[32,2304]{1,0:T(8,128)(2,1)S(1)} all-gather(bf16[8,2304]{1,0:T(8,128)(2,1)S(1)} %get-tuple-element.24), channel_id=1, replica_groups=mesh['section'=8,'dp'=4] {'dp'}, dimensions={0}, use_global_device_ids=true | all-gather | bytes 184320 | tf_op jit(solution)/shard_map/all_gather | solution.py:138
  177.0 5.5 %fusion.243 = f32[1152,2304]{1,0:T(8,128)} fusion(bf16[32,2304]{1,0:T(8,128)(2,1)S(1)} %all_gather.46, f32[32,1152]{1,0:T(8,128)S(1)} %fusion.52), kind=kOutput, calls=%fused_computation.241 | convolution fusion | flops 170201088 | bytes 10911744 | tf_op jit(solution)/shard_map/dot_general | solution.py:45
  182.5 9.5 %convolution_add_fusion = f32[1152,2304]{1,0:T(8,128)} fusion(f32[1152,2304]{1,0:T(8,128)} %fusion.243, bf16[32,2304]{1,0:T(8,128)(2,1)S(1)} %all_gather.42, f32[32,1152]{1,0:T(8,128)S(1)} %fusion.117, f32[32,1152]{1,0:T(8,128)S(1)} %fusion.52), kind=kOutput, calls=%fused_computation | convolution fusion | flops 173223936 | bytes 21676032 | tf_op jit(solution)/shard_map/dot_general | solution.py:45
  193.8 5.6 %convolution_add_fusion.2 = f32[2304,1152]{1,0:T(8,128)} fusion(f32[2304,1152]{1,0:T(8,128)S(1)} %fusion.305, bf16[32,2304]{1,0:T(8,128)(2,1)S(1)} %all_gather.43, bf16[32,1152]{1,0:T(8,128)(2,1)S(1)} %fusion.138), kind=kOutput, calls=%fused_computation.2 | convolution fusion | flops 172523520 | bytes 21454848 | tf_op jit(solution)/shard_map/dot_general | solution.py:45
  201.7 11.1 %fusion.5 = bf16[1,1152,2304]{2,1,0:T(8,128)(2,1)} fusion(f32[1152,2304]{1,0:T(8,128)} %convolution_add_fusion, f32[1152,2304]{1,0:T(8,128)} %fusion.242, bf16[32,2304]{1,0:T(8,128)(2,1)S(1)} %all_gather.40, f32[32,1152]{1,0:T(8,128)S(1)} %fusion.114, f32[32,1152]{1,0:T(8,128)S(1)} %fusion.56), kind=kOutput, calls=%fused_computation.9 | convolution fusion | flops 178532352 | bytes 26984448 | tf_op jit(solution)/shard_map/dot_general | solution.py:45
  217.5 11.0 %fusion.4 = bf16[1,2304,1152]{2,1,0:T(8,128)(2,1)} fusion(f32[2304,1152]{1,0:T(8,128)} %convolution_add_fusion.2, f32[2304,1152]{1,0:T(8,128)} %fusion.304, bf16[32,2304]{1,0:T(8,128)(2,1)S(1)} %all_gather.41, bf16[32,1152]{1,0:T(8,128)(2,1)S(1)} %fusion.141), kind=kOutput, calls=%fused_computation.8 | convolution fusion | flops 177831936 | bytes 26763264 | tf_op jit(solution)/shard_map/dot_general | solution.py:45
  228.5 15.4 %reduce-scatter.19.cloned.1.call-done = bf16[8,2304]{1,0:T(8,128)(2,1)} async-done(((bf16[32,2304]{1,0:T(8,128)(2,1)}), bf16[8,2304]{1,0:T(8,128)(2,1)}) %reduce-scatter.19.cloned.1.call-update) | async-done | bytes 36880 | tf_op jit(solution)/shard_map/reduce_scatter | solution.py:155
  245.0 5.8 %all_gather.36 = bf16[32,2304]{1,0:T(8,128)(2,1)S(1)} all-gather(bf16[8,2304]{1,0:T(8,128)(2,1)S(1)} %get-tuple-element.38), channel_id=1, replica_groups=mesh['section'=8,'dp'=4] {'dp'}, dimensions={0}, use_global_device_ids=true | all-gather | bytes 184320 | tf_op jit(solution)/shard_map/all_gather | solution.py:133
  264.2 6.7 %fusion.81 = bf16[32,2304]{1,0:T(8,128)(2,1)} fusion(f32[32,2304]{1,0:T(8,128)S(1)} %fusion.12, bf16[1,1152,2304]{2,1,0:T(8,128)(2,1)} %param.23, f32[32,1152]{1,0:T(8,128)S(1)} %fusion.24, bf16[32,2304]{1,0:T(8,128)(2,1)S(1)} %all_gather.38, bf16[1,2304,1152]{2,1,0:T(8,128)(2,1)} %param.22, f32[32,1152]{1,0:T(8,128)S(1)} %fusion.64), kind=kOutput, calls=%fused_computation.75 | convolution fusion | flops 340623360 | bytes 11501568 | tf_op jit(solution)/shard_map/dot_general | solution.py:35
  275.0 15.7 %reduce-scatter.13.cloned.1.call-done = bf16[8,2304]{1,0:T(8,128)(2,1)} async-done(((bf16[32,2304]{1,0:T(8,128)(2,1)}), bf16[8,2304]{1,0:T(8,128)(2,1)}) %reduce-scatter.13.cloned.1.call-update) | async-done | bytes 36880 | tf_op jit(solution)/shard_map/reduce_scatter | solution.py:150
  294.9 17.8 %reduce-scatter.9.cloned.1.call-done = bf16[8,2304]{1,0:T(8,128)(2,1)} async-done(((bf16[32,2304]{1,0:T(8,128)(2,1)}), bf16[8,2304]{1,0:T(8,128)(2,1)}) %reduce-scatter.9.cloned.1.call-update) | async-done | bytes 36880 | tf_op jit(solution)/shard_map/reduce_scatter | solution.py:147
  319.5 5.6 %all_gather.37 = bf16[32,2304]{1,0:T(8,128)(2,1)S(1)} all-gather(bf16[8,2304]{1,0:T(8,128)(2,1)S(1)} %get-tuple-element.36), channel_id=1, replica_groups=mesh['section'=8,'dp'=4] {'dp'}, dimensions={0}, use_global_device_ids=true | all-gather | bytes 184320 | tf_op jit(solution)/shard_map/all_gather | solution.py:133
  338.5 6.7 %fusion.78 = bf16[32,2304]{1,0:T(8,128)(2,1)} fusion(f32[32,2304]{1,0:T(8,128)S(1)} %fusion.10, bf16[1,1152,2304]{2,1,0:T(8,128)(2,1)} %param.23, f32[32,1152]{1,0:T(8,128)S(1)} %fusion.22, bf16[32,2304]{1,0:T(8,128)(2,1)S(1)} %all_gather.39, bf16[1,2304,1152]{2,1,0:T(8,128)(2,1)} %param.22, f32[32,1152]{1,0:T(8,128)S(1)} %fusion.62), kind=kOutput, calls=%fused_computation.74 | convolution fusion | flops 340623360 | bytes 11501568 | tf_op jit(solution)/shard_map/dot_general | solution.py:35
  349.3 16.6 %reduce-scatter.15.cloned.1.call-done = bf16[8,2304]{1,0:T(8,128)(2,1)} async-done(((bf16[32,2304]{1,0:T(8,128)(2,1)}), bf16[8,2304]{1,0:T(8,128)(2,1)}) %reduce-scatter.15.cloned.1.call-update) | async-done | bytes 36880 | tf_op jit(solution)/shard_map/reduce_scatter | solution.py:150
  367.3 20.7 %reduce-scatter.11.cloned.1.call-done = bf16[8,2304]{1,0:T(8,128)(2,1)} async-done(((bf16[32,2304]{1,0:T(8,128)(2,1)}), bf16[8,2304]{1,0:T(8,128)(2,1)}) %reduce-scatter.11.cloned.1.call-update) | async-done | bytes 36880 | tf_op jit(solution)/shard_map/reduce_scatter | solution.py:147
  (147 shorter events, 133.5 us)
Async XLA Ops:
  7.2 89.8 %reduce-scatter.21.cloned.1.call-start = ((), (), s32[]{:S(2)}) async-start(), calls=%async_computation.14 | async-start | bytes 184320 | tf_op jit(solution)/shard_map/reduce_scatter | solution.py:158
  7.2 31.2 %copy-start = (bf16[1,2304,1152]{2,1,0:T(8,128)(2,1)S(1)}, bf16[1,2304,1152]{2,1,0:T(8,128)(2,1)}, u32[]{:S(2)}) copy-start(bf16[1,2304,1152]{2,1,0:T(8,128)(2,1)} %param.22) | copy-start | bytes 15925252
  7.2 33.2 %collective-permute-start.4 = (bf16[8,2304]{1,0:T(8,128)(2,1)}, bf16[8,2304]{1,0:T(8,128)(2,1)S(1)}, u32[]{:S(2)}, u32[]{:S(2)}) collective-permute-start(bf16[8,2304]{1,0:T(8,128)(2,1)} %bitcast.244), channel_id=1, source_target_pairs={{4,0},{8,4},{12,8},{16,12},{20,16},{24,20},{28,24},{5,1},{9,5},{13... | collective-permute-start | bytes 110600 | tf_op jit(solution)/shard_map/ppermute | solution.py:17
  8.8 52.8 %collective-permute-start.6 = (bf16[8,2304]{1,0:T(8,128)(2,1)}, bf16[8,2304]{1,0:T(8,128)(2,1)S(1)}, u32[]{:S(2)}, u32[]{:S(2)}) collective-permute-start(bf16[8,2304]{1,0:T(8,128)(2,1)} %bitcast.245), channel_id=1, source_target_pairs={{4,0},{8,4},{12,8},{16,12},{20,16},{24,20},{28,24},{5,1},{9,5},{13... | collective-permute-start | bytes 110600 | tf_op jit(solution)/shard_map/ppermute | solution.py:17
  10.1 71.5 %collective-permute-start.2 = (bf16[8,2304]{1,0:T(8,128)(2,1)}, bf16[8,2304]{1,0:T(8,128)(2,1)S(1)}, u32[]{:S(2)}, u32[]{:S(2)}) collective-permute-start(bf16[8,2304]{1,0:T(8,128)(2,1)} %bitcast.246), channel_id=1, source_target_pairs={{0,4},{4,8},{8,12},{12,16},{16,20},{20,24},{24,28},{1,5},{5,9},{9,... | collective-permute-start | bytes 110600 | tf_op jit(solution)/shard_map/ppermute | solution.py:17
  16.4 65.3 %collective-permute-start = (bf16[8,2304]{1,0:T(8,128)(2,1)}, bf16[8,2304]{1,0:T(8,128)(2,1)S(1)}, u32[]{:S(2)}, u32[]{:S(2)}) collective-permute-start(bf16[8,2304]{1,0:T(8,128)(2,1)} %bitcast.247), channel_id=1, source_target_pairs={{0,4},{4,8},{8,12},{12,16},{16,20},{20,24},{24,28},{1,5},{5,9},{9,... | collective-permute-start | bytes 110600 | tf_op jit(solution)/shard_map/ppermute | solution.py:17
  74.5 45.3 %copy-start.1 = (bf16[1,2,8,2304]{3,2,1,0:T(8,128)(2,1)S(1)}, bf16[1,2,8,2304]{3,2,1,0:T(8,128)(2,1)}, u32[]{:S(2)}) copy-start(bf16[1,2,8,2304]{3,2,1,0:T(8,128)(2,1)} %param.19) | copy-start | bytes 221188
  74.5 45.3 %copy-start.2 = (bf16[1,2,8,2304]{3,2,1,0:T(8,128)(2,1)S(1)}, bf16[1,2,8,2304]{3,2,1,0:T(8,128)(2,1)}, u32[]{:S(2)}) copy-start(bf16[1,2,8,2304]{3,2,1,0:T(8,128)(2,1)} %param.20) | copy-start | bytes 221188
  76.7 43.0 %reduce-scatter.17.cloned.1.call-start = ((), (), s32[]{:S(2)}) async-start(), calls=%async_computation.12 | async-start | bytes 184320 | tf_op jit(solution)/shard_map/reduce_scatter | solution.py:155
  81.5 72.9 %slice-start.2 = ((s8[5308416]{0:T(1024)(128)(4,1)}), s8[1114112]{0:T(1024)(128)(4,1)S(1)}, s32[]{:S(2)}) async-start(s8[5308416]{0:T(1024)(128)(4,1)} %bitcast.228), calls=%async_computation.18 | async-start | bytes 2228224
  81.5 147.0 %reduce-scatter.23.cloned.1.call-start = ((), (), s32[]{:S(2)}) async-start(), calls=%async_computation.15 | async-start | bytes 184320 | tf_op jit(solution)/shard_map/reduce_scatter | solution.py:158
  138.5 26.6 %slice-start.12 = ((s8[5308416]{0:T(1024)(128)(4,1)}), s8[4194304]{0:T(1024)(128)(4,1)S(1)}, s32[]{:S(2)}) async-start(s8[5308416]{0:T(1024)(128)(4,1)} %bitcast.238), calls=%async_computation.28 | async-start | bytes 8388608
  142.2 22.9 %slice-start.13 = ((s8[5308416]{0:T(1024)(128)(4,1)}), s8[1114112]{0:T(1024)(128)(4,1)S(1)}, s32[]{:S(2)}) async-start(s8[5308416]{0:T(1024)(128)(4,1)} %bitcast.238), calls=%async_computation.29 | async-start | bytes 2228224
  146.0 25.5 %collective-permute-start.7 = (bf16[8,2304]{1,0:T(8,128)(2,1)S(1)}, bf16[8,2304]{1,0:T(8,128)(2,1)S(1)}, u32[]{:S(2)}, u32[]{:S(2)}) collective-permute-start(bf16[8,2304]{1,0:T(8,128)(2,1)S(1)} %get-tuple-element.25), channel_id=1, source_target_pairs={{4,0},{8,4},{12,8},{16,12},{20,16},{24,20},{28,24},{5,1},{9,5},{13... | collective-permute-start | bytes 110600 | tf_op jit(solution)/shard_map/ppermute | solution.py:17
  153.0 6.6 %collective-permute-start.5 = (bf16[8,2304]{1,0:T(8,128)(2,1)S(1)}, bf16[8,2304]{1,0:T(8,128)(2,1)S(1)}, u32[]{:S(2)}, u32[]{:S(2)}) collective-permute-start(bf16[8,2304]{1,0:T(8,128)(2,1)S(1)} %get-tuple-element.26), channel_id=1, source_target_pairs={{4,0},{8,4},{12,8},{16,12},{20,16},{24,20},{28,24},{5,1},{9,5},{13... | collective-permute-start | bytes 110600 | tf_op jit(solution)/shard_map/ppermute | solution.py:17
  201.6 42.3 %reduce-scatter.19.cloned.1.call-start = ((), (), s32[]{:S(2)}) async-start(), calls=%async_computation.13 | async-start | bytes 184320 | tf_op jit(solution)/shard_map/reduce_scatter | solution.py:155
  217.5 73.3 %reduce-scatter.13.cloned.1.call-start = ((), (), s32[]{:S(2)}) async-start(), calls=%async_computation.10 | async-start | bytes 184320 | tf_op jit(solution)/shard_map/reduce_scatter | solution.py:150
  270.9 47.8 %copy-start.3 = (bf16[8,2304]{1,0:T(8,128)(2,1)S(1)}, bf16[8,2304]{1,0:T(8,128)(2,1)}, u32[]{:S(2)}) copy-start(bf16[8,2304]{1,0:T(8,128)(2,1)} %reduce-scatter.23.cloned.1.call-done) | copy-start | bytes 110596
  270.9 47.8 %copy-start.4 = (bf16[8,2304]{1,0:T(8,128)(2,1)S(1)}, bf16[8,2304]{1,0:T(8,128)(2,1)}, u32[]{:S(2)}) copy-start(bf16[8,2304]{1,0:T(8,128)(2,1)} %reduce-scatter.19.cloned.1.call-done) | copy-start | bytes 110596
  270.9 41.8 %reduce-scatter.9.cloned.1.call-start = ((), (), s32[]{:S(2)}) async-start(), calls=%async_computation.8 | async-start | bytes 184320 | tf_op jit(solution)/shard_map/reduce_scatter | solution.py:147
  275.0 90.9 %reduce-scatter.15.cloned.1.call-start = ((), (), s32[]{:S(2)}) async-start(), calls=%async_computation.11 | async-start | bytes 184320 | tf_op jit(solution)/shard_map/reduce_scatter | solution.py:150
  291.5 25.4 %collective-permute-start.3 = (bf16[8,2304]{1,0:T(8,128)(2,1)S(1)}, bf16[8,2304]{1,0:T(8,128)(2,1)S(1)}, u32[]{:S(2)}, u32[]{:S(2)}) collective-permute-start(bf16[8,2304]{1,0:T(8,128)(2,1)S(1)} %fusion.213), channel_id=1, source_target_pairs={{0,4},{4,8},{8,12},{12,16},{16,20},{20,24},{24,28},{1,5},{5,9},{9,... | collective-permute-start | bytes 110600 | tf_op jit(solution)/shard_map/ppermute | solution.py:17
  313.5 5.0 %collective-permute-start.1 = (bf16[8,2304]{1,0:T(8,128)(2,1)S(1)}, bf16[8,2304]{1,0:T(8,128)(2,1)S(1)}, u32[]{:S(2)}, u32[]{:S(2)}) collective-permute-start(bf16[8,2304]{1,0:T(8,128)(2,1)S(1)} %fusion.235), channel_id=1, source_target_pairs={{0,4},{4,8},{8,12},{12,16},{16,20},{20,24},{24,28},{1,5},{5,9},{9,... | collective-permute-start | bytes 110600 | tf_op jit(solution)/shard_map/ppermute | solution.py:17
  345.2 42.8 %reduce-scatter.11.cloned.1.call-start = ((), (), s32[]{:S(2)}) async-start(), calls=%async_computation.9 | async-start | bytes 184320 | tf_op jit(solution)/shard_map/reduce_scatter | solution.py:147
  (17 other events, 158.3 us)
Sparse Core Ops, SparseCore 0:
  76.9 20.0 reduce-scatter.20
  100.0 19.6 reduce-scatter.16
  201.7 20.1 reduce-scatter.22
  224.2 19.6 reduce-scatter.18
  271.0 19.6 reduce-scatter.12
  293.0 19.6 reduce-scatter.8
  345.4 20.5 reduce-scatter.14
  368.4 19.6 reduce-scatter.10
where the time goes:
time: 400 us; the launch traced here: 397 us
  matrix products  139 us (35%)
  waiting for transfers between devices  130 us (32%)
  blocking collectives  77.8 us (19%)
  starting transfers between devices  23.7 us (6%)
  between operations  15.1 us (4%)
  other arithmetic  11.1 us (3%)
    dot_general x8, matrix products, product_first(): lax.dot_general(left, right, (((0,), (0,)), ((), ())), preferred_element_...  55.4 us
    dot_general x16, matrix products, matrix_product(): return jnp.dot(left, right, preferred_element_type=jnp.float32)  51.3 us
    reduce_scatter x2, waiting for transfers between devices, reduce_rows(): lax.psum_scatter(forward_term.astype(jnp.bfloat16), 'dp', scatter_dimensi...  38.6 us
    reduce_scatter x2, waiting for transfers between devices, reduce_rows(): lax.psum_scatter(backward_term.astype(jnp.bfloat16), 'dp', scatter_dimens...  38.1 us
    reduce_scatter x2, waiting for transfers between devices, reduce_rows(): lax.psum_scatter(forward_tan.astype(jnp.bfloat16), 'dp', scatter_dimensio...  32.3 us
    dot_general x12, matrix products, product_last(): lax.dot_general(left, right, (((1,), (1,)), ((), ())), preferred_element_...  32.1 us
    ppermute x8, starting transfers between devices, passed_along(): lax.ppermute(value, axis, [(source, source + steps) for source in range(l...  23.4 us
    all_gather x2, blocking collectives, gather_rows(): lax.all_gather(stash_rows, 'dp', axis=0, tiled=True)  22.4 us
  transfers between devices with their start and end apart: 16, of which 9 were waited for; matrix products, arithmetic and copies ran while one was open for 21% of the time, Pallas kernels for 0%

commit v1 on v0

v1 whole, which is shorter than its diff:
```python
import functools

import jax
import jax.numpy as jnp
from jax import lax
from jax.experimental import pallas as pl
from jax.experimental.pallas import tpu as pltpu
from jax.sharding import PartitionSpec as P

sqrt_two_over_pi = 0.7978845608028654
cubic_coef = 0.044715
norm_eps = 1e-06


def gelu_parts(linear):
    inner_arg = sqrt_two_over_pi * (linear + cubic_coef * linear * linear * linear)
    first_slope = sqrt_two_over_pi * (1.0 + 3.0 * cubic_coef * linear * linear)
    second_slope = 6.0 * sqrt_two_over_pi * cubic_coef * linear
    tanh_value = jnp.tanh(inner_arg)
    sech_square = 1.0 - tanh_value * tanh_value
    gelu_value = 0.5 * linear * (1.0 + tanh_value)
    gelu_first = 0.5 * (1.0 + tanh_value) + 0.5 * linear * sech_square * first_slope
    gelu_second = sech_square * (
        first_slope - linear * tanh_value * first_slope * first_slope + 0.5 * linear * second_slope
    )
    return (gelu_value, gelu_first, gelu_second)


def matrix_product(left, right):
    return jnp.dot(left, right, preferred_element_type=jnp.float32)


def product_last(left, right):
    return lax.dot_general(
        left, right, (((1,), (1,)), ((), ())), preferred_element_type=jnp.float32
    )


def product_first(left, right):
    return lax.dot_general(
        left, right, (((0,), (0,)), ((), ())), preferred_element_type=jnp.float32
    )


f32, bf16 = (jnp.float32, jnp.bfloat16)
MESH = pl.DeviceIdType.MESH


def lane_chunk(size, wanted):
    fits = [c for c in range(128, wanted + 1, 128) if size % c == 0]
    return max(fits) if fits else size


def over_chunks(size, chunk, body):
    if size == chunk:
        body(pl.ds(0, size))
        return

    def step(index, carry):
        body(pl.ds(pl.multiple_of(index * chunk, chunk), chunk))
        return carry

    lax.fori_loop(0, size // chunk, step, 0)


def pair(value, tangent):
    blocks, rows, width = value.shape
    return jnp.stack([value, tangent], axis=1).reshape(blocks * 2 * rows, width)


def unpair(stacked, rows):
    wide = stacked.astype(f32).reshape(-1, 2, rows, stacked.shape[-1])
    return (wide[:, 0], wide[:, 1])


def norm_pair(stacked, gain, rows):
    values, values_tan = unpair(stacked, rows)
    inverse = lax.rsqrt(jnp.mean(values * values, axis=-1, keepdims=True) + norm_eps)
    inverse_tan = -(inverse * inverse * inverse) * jnp.mean(
        values * values_tan, axis=-1, keepdims=True
    )
    return (values * inverse * gain, (values_tan * inverse + values * inverse_tan) * gain)


def relay_kernel(
    sections, n_dp, ticks,
    carry_act, carry_act_tan, carry_adj, carry_adj_tan, fresh_act, loss_cot, stash_act,
    stash_act_tan, norm_gain, up_hbm, down_hbm, up_dir_hbm, down_dir_hbm,
    stash_out, adj_out, hidden_out, delta_out, final_out,
    up, down, up_dir, down_dir,
    left, left_dir, hid, hid_dir, slope, bend, hid_swap, delta, delta_dir, delta_swap,
    adj_dir, stash_all, gathered, outgoing, partial, from_core, to_chip, from_chip,
    weight_sems, out_sems, core_sems, chip_sems, shift_sems, relay_sems, stash_sems, stash_relay,
):
    chips = n_dp // 2
    rows = carry_act.shape[1]
    width = carry_act.shape[2]
    units = up.shape[1]
    band = n_dp * 2 * rows
    section, part = (lax.axis_index("section"), lax.axis_index("dp"))
    chip, core = (part // 2, part % 2)
    other = 1 - core
    after, before = (lax.rem(section + 1, sections), lax.rem(section + sections - 1, sections))
    partner = (section, chip * 2 + other)
    gain = norm_gain[...].astype(f32)

    def chip_at(step):
        return lax.rem(chip + step, chips)

    loads = [
        pltpu.make_async_copy(source.at[0], target, weight_sems.at[i])
        for i, (source, target) in enumerate(
            ((up_hbm, up), (up_dir_hbm, up_dir), (down_hbm, down), (down_dir_hbm, down_dir))
        )
    ]
    for load in loads:
        load.start()

    barrier = pltpu.get_barrier_semaphore()
    pl.semaphore_signal(barrier, inc=1, device_id=partner, device_id_type=MESH)
    for step in range(chips):
        place = chip_at(step) * 2 + core
        for where in (after, before):
            pl.semaphore_signal(barrier, inc=1, device_id=(where, place), device_id_type=MESH)
        if step:
            pl.semaphore_signal(barrier, inc=1, device_id=(section, place), device_id_type=MESH)

    def shift_copies(lane):
        where = after if lane % 2 == 0 else before
        return [
            pltpu.make_async_remote_copy(
                src_ref=outgoing.at[lane],
                dst_ref=gathered.at[lane, core, chip],
                send_sem=shift_sems.at[lane, 0, step],
                recv_sem=shift_sems.at[lane, 1, step],
                device_id=(where, chip_at(step) * 2 + core),
                device_id_type=MESH,
            )
            for step in range(chips)
        ]

    def relay_copy(lane):
        return pltpu.make_async_remote_copy(
            src_ref=gathered.at[lane, core],
            dst_ref=gathered.at[lane, core],
            send_sem=relay_sems.at[lane, 0],
            recv_sem=relay_sems.at[lane, 1],
            device_id=partner,
            device_id_type=MESH,
        )

    def stash_copies():
        return [
            pltpu.make_async_remote_copy(
                src_ref=stash_all.at[core, chip],
                dst_ref=stash_all.at[core, chip],
                send_sem=stash_sems.at[0, step],
                recv_sem=stash_sems.at[1, step],
                device_id=(section, chip_at(step) * 2 + core),
                device_id_type=MESH,
            )
            for step in range(1, chips)
        ]

    def stash_relay_copy():
        return pltpu.make_async_remote_copy(
            src_ref=stash_all.at[core],
            dst_ref=stash_all.at[core],
            send_sem=stash_relay.at[0],
            recv_sem=stash_relay.at[1],
            device_id=partner,
            device_id_type=MESH,
        )

    def core_copy(lane):
        return pltpu.make_async_remote_copy(
            src_ref=partial.at[lane, other],
            dst_ref=from_core.at[lane],
            send_sem=core_sems.at[lane, 0],
            recv_sem=core_sems.at[lane, 1],
            device_id=partner,
            device_id_type=MESH,
        )

    def chip_copies(lane):
        return [
            pltpu.make_async_remote_copy(
                src_ref=to_chip.at[lane, step - 1],
                dst_ref=from_chip.at[lane, step - 1],
                send_sem=chip_sems.at[lane, 0, step - 1],
                recv_sem=chip_sems.at[lane, 1, step - 1],
                device_id=(section, chip_at(step) * 2 + core),
                device_id_type=MESH,
            )
            for step in range(1, chips)
        ]

    def start_all(copies):
        for copy in copies:
            copy.start()

    def stage_shift(lane, value, tangent):
        tick = lane // 2
        if lane % 2 == 0:
            ends, entering = (section == sections - 1, fresh_act[tick])
        else:
            ends, entering = (section == 0, loss_cot[tick])
        value = jnp.where(ends, entering.astype(f32), value)
        tangent = jnp.where(ends, 0.0, tangent)
        outgoing[lane] = pair(value[None], tangent[None]).astype(bf16)

    def relay(lane):
        for copy in shift_copies(lane):
            copy.wait_recv()
        relay_copy(lane).start()

    def reduce_in_chip(lane):
        core_copy(lane).wait_recv()
        for step in range(1, chips):
            place = chip_at(step)
            summed = partial[lane, core, place].astype(f32) + from_core[lane, place].astype(f32)
            to_chip[lane, step - 1] = summed.astype(bf16)
        start_all(chip_copies(lane))

    def reduced(lane):
        total = partial[lane, core, chip].astype(f32) + from_core[lane, chip].astype(f32)
        for step, copy in enumerate(chip_copies(lane)):
            copy.wait_recv()
            total = total + from_chip[lane, step].astype(f32)
        return (total[:rows], total[rows:])

    stage_shift(0, carry_act[0].astype(f32), carry_act_tan[0].astype(f32))
    pl.semaphore_wait(barrier, 3 * chips)
    start_all(shift_copies(0))
    stage_shift(1, carry_adj[0].astype(f32), carry_adj_tan[0].astype(f32))
    start_all(shift_copies(1))
    for tick in range(ticks):
        stacked = pair(
            stash_act[0, tick].astype(f32)[None], stash_act_tan[0, tick].astype(f32)[None]
        )
        normed, normed_tan = norm_pair(stacked, gain, rows)
        stash_all[core, chip, tick] = pair(normed, normed_tan).astype(bf16)
    start_all(stash_copies())
    relay(0)
    relay(1)
    for copy in stash_copies():
        copy.wait_recv()
    stash_relay_copy().start()

    outs = []

    def send_out(source, target):
        copy = pltpu.make_async_copy(source, target, out_sems.at[len(outs)])
        copy.start()
        outs.append(copy)

    def stage_forward(tick):
        lane = 2 * tick
        relay_copy(lane).wait_recv()
        for block in range(n_dp):
            where = pl.ds(block * 2 * rows, 2 * rows)
            normed, normed_tan = norm_pair(
                gathered[lane, block // chips, block % chips], gain, rows
            )
            left[where, :] = pair(normed, normed_tan).astype(bf16)
            left_dir[where, :] = pair(jnp.zeros_like(normed), normed).astype(bf16)

    stage_forward(0)
    stash_relay_copy().wait_recv()
    for block in range(n_dp):
        for tick in range(ticks):
            where = pl.ds(band + (block * ticks + tick) * 2 * rows, 2 * rows)
            stacked = stash_all[block // chips, block % chips, tick]
            left[where, :] = stacked
            value = unpair(stacked, rows)[0]
            left_dir[where, :] = pair(jnp.zeros_like(value), value).astype(bf16)
    send_out(stash_all, stash_out)
    loads[0].wait()
    loads[1].wait()

    unit_chunk = lane_chunk(units, 384)
    width_chunk = lane_chunk(width, 768)

    def up_products(height, with_stash, cols):
        stacked = matrix_product(left[:height, :], up[:, cols]) + matrix_product(
            left_dir[:height, :], up_dir[:, cols]
        )
        linear, linear_tan = unpair(stacked[:band], rows)
        value, first, _ = gelu_parts(linear)
        hid[:, cols] = pair(value, first * linear_tan).astype(bf16)
        hid_dir[:, cols] = pair(jnp.zeros_like(value), value).astype(bf16)
        if with_stash:
            linear, linear_tan = unpair(stacked[band:], rows)
            value, first, second = gelu_parts(linear)
            hid_swap[:, cols] = pair(first * linear_tan, value).astype(bf16)
            by_tick = (n_dp, ticks, rows, value.shape[-1])
            slope[:, :, :, cols] = first.reshape(by_tick)
            bend[:, :, :, cols] = (second * linear_tan).reshape(by_tick)

    def down_products(lane, cols):
        stacked = matrix_product(hid[...], down[:, cols]) + matrix_product(
            hid_dir[...], down_dir[:, cols]
        )
        partial[lane, :, :, :, cols] = stacked.astype(bf16).reshape(2, chips, 2 * rows, -1)

    def adjoint_products(tick, cols):
        adjoint = gathered[2 * tick + 1].reshape(band, width)
        stacked = product_last(adjoint, down[cols, :]) + product_last(
            adj_dir[...], down_dir[cols, :]
        )
        upstream, upstream_tan = unpair(stacked, rows)
        first, second_tan = (slope[:, tick, :, cols], bend[:, tick, :, cols])
        value = upstream * first
        tangent = upstream_tan * first + upstream * second_tan
        delta[:, cols] = pair(value, tangent).astype(bf16)
        delta_dir[:, cols] = pair(jnp.zeros_like(value), value).astype(bf16)
        delta_swap[:, tick, :, cols] = (
            pair(tangent, value).astype(bf16).reshape(n_dp, 2 * rows, -1)
        )

    def back_products(lane, cols):
        stacked = product_last(delta[...], up[cols, :]) + product_last(
            delta_dir[...], up_dir[cols, :]
        )
        partial[lane, :, :, :, cols] = stacked.astype(bf16).reshape(2, chips, 2 * rows, -1)

    def finish_forward(tick):
        lane = 2 * tick
        value, tangent = reduced(lane)
        own = gathered[lane, core, chip].astype(f32)
        value, tangent = (own[:rows] + value, own[rows:] + tangent)
        if tick + 1 < ticks:
            stage_shift(lane + 2, value, tangent)
            start_all(shift_copies(lane + 2))
        else:
            final_out[0] = value.astype(bf16)
            final_out[1] = tangent.astype(bf16)

    def finish_backward(tick):
        lane = 2 * tick + 1
        summed, summed_tan = reduced(lane)
        arriving = gathered[lane, core, chip].astype(f32)
        values = stash_act[0, tick].astype(f32)
        values_tan = stash_act_tan[0, tick].astype(f32)
        inverse = lax.rsqrt(jnp.mean(values * values, axis=-1, keepdims=True) + norm_eps)
        cube = inverse * inverse * inverse
        inverse_tan = -cube * jnp.mean(values * values_tan, axis=-1, keepdims=True)
        weighted, weighted_tan = (summed * gain, summed_tan * gain)
        moment = jnp.mean(values * weighted, axis=-1, keepdims=True)
        moment_tan = jnp.mean(
            values_tan * weighted + values * weighted_tan, axis=-1, keepdims=True
        )
        value = arriving[:rows] + inverse * weighted - cube * values * moment
        tangent = (
            arriving[rows:]
            + inverse_tan * weighted
            + inverse * weighted_tan
            - 3.0 * inverse * inverse * inverse_tan * values * moment
            - cube * values_tan * moment
            - cube * values * moment_tan
        )
        if tick + 1 < ticks:
            stage_shift(lane + 2, value, tangent)
            start_all(shift_copies(lane + 2))
        else:
            final_out[2] = value.astype(bf16)
            final_out[3] = tangent.astype(bf16)

    for tick in range(ticks):
        ahead, behind = (2 * tick, 2 * tick + 1)
        if tick:
            stage_forward(tick)
        height = left.shape[0] if tick == 0 else band
        over_chunks(units, unit_chunk, functools.partial(up_products, height, tick == 0))
        if tick == 0:
            send_out(hid_swap, hidden_out)
            loads[2].wait()
            loads[3].wait()
        else:
            relay(behind)
        over_chunks(width, width_chunk, functools.partial(down_products, ahead))
        core_copy(ahead).start()
        relay_copy(behind).wait_recv()
        for block in range(n_dp):
            value = unpair(gathered[behind, block // chips, block % chips], rows)[0]
            adj_dir[pl.ds(block * 2 * rows, 2 * rows), :] = pair(
                jnp.zeros_like(value), value
            ).astype(bf16)
        send_out(gathered.at[behind], adj_out.at[tick])
        over_chunks(units, unit_chunk, functools.partial(adjoint_products, tick))
        reduce_in_chip(ahead)
        over_chunks(width, width_chunk, functools.partial(back_products, behind))
        core_copy(behind).start()
        finish_forward(tick)
        reduce_in_chip(behind)
        if tick + 1 < ticks:
            relay(ahead + 2)
        else:
            send_out(delta_swap, delta_out)
        finish_backward(tick)

    for lane in range(2 * ticks):
        for copy in shift_copies(lane) + chip_copies(lane):
            copy.wait_send()
        relay_copy(lane).wait_send()
        core_copy(lane).wait_send()
    for copy in stash_copies():
        copy.wait_send()
    stash_relay_copy().wait_send()
    for copy in outs:
        copy.wait()


def curvature_kernel(split_units, stash_sw, delta_sw, hidden_sw, adj, final, *outs):
    act, act_tan, adj_new, adj_new_tan, up_out, down_out = outs
    for index, target in enumerate((act, act_tan, adj_new, adj_new_tan)):
        target[0] = final[index]
    up_out[0] = product_first(stash_sw[...], delta_sw[...]).astype(bf16)

    def down():
        down_out[0] = product_first(hidden_sw[...], adj[...]).astype(bf16)

    if split_units:
        down()
    else:
        pl.when(pl.program_id(0) == 0)(down)


def shards(
    carry_act, carry_act_tan, carry_adj, carry_adj_tan, fresh_act, loss_cot, stash_act,
    stash_act_tan, norm_gain, up_weight, down_weight, up_dir, down_dir,
):
    sections, n_dp = (lax.axis_size("section"), lax.axis_size("dp"))
    chips = n_dp // 2
    ticks, rows, width = fresh_act.shape
    units = up_weight.shape[2]
    band = n_dp * 2 * rows
    tall = band * (1 + ticks)
    lanes = 2 * ticks
    vmem, anywhere = (
        pl.BlockSpec(memory_space=pltpu.VMEM),
        pl.BlockSpec(memory_space=pl.ANY),
    )
    block = (2 * rows, width)
    stash_out, adj_out, hidden_out, delta_out, final_out = pl.pallas_call(
        functools.partial(relay_kernel, sections, n_dp, ticks),
        out_shape=(
            jax.ShapeDtypeStruct((2, chips, ticks) + block, bf16),
            jax.ShapeDtypeStruct((ticks, 2, chips) + block, bf16),
            jax.ShapeDtypeStruct((band * ticks, units), bf16),
            jax.ShapeDtypeStruct((n_dp, ticks, 2 * rows, units), bf16),
            jax.ShapeDtypeStruct((4, rows, width), bf16),
        ),
        in_specs=[vmem] * 9 + [anywhere] * 4,
        out_specs=(anywhere,) * 4 + (vmem,),
        scratch_shapes=[
            pltpu.VMEM((width, units), bf16),
            pltpu.VMEM((units, width), bf16),
            pltpu.VMEM((width, units), bf16),
            pltpu.VMEM((units, width), bf16),
            pltpu.VMEM((tall, width), bf16),
            pltpu.VMEM((tall, width), bf16),
            pltpu.VMEM((band, units), bf16),
            pltpu.VMEM((band, units), bf16),
            pltpu.VMEM((n_dp, ticks, rows, units), f32),
            pltpu.VMEM((n_dp, ticks, rows, units), f32),
            pltpu.VMEM((band * ticks, units), bf16),
            pltpu.VMEM((band, units), bf16),
            pltpu.VMEM((band, units), bf16),
            pltpu.VMEM((n_dp, ticks, 2 * rows, units), bf16),
            pltpu.VMEM((band, width), bf16),
            pltpu.VMEM((2, chips, ticks) + block, bf16),
            pltpu.VMEM((lanes, 2, chips) + block, bf16),
            pltpu.VMEM((lanes,) + block, bf16),
            pltpu.VMEM((lanes, 2, chips) + block, bf16),
            pltpu.VMEM((lanes, chips) + block, bf16),
            pltpu.VMEM((lanes, chips - 1) + block, bf16),
            pltpu.VMEM((lanes, chips - 1) + block, bf16),
            pltpu.SemaphoreType.DMA((4,)),
            pltpu.SemaphoreType.DMA((3 + ticks,)),
            pltpu.SemaphoreType.DMA((lanes, 2)),
            pltpu.SemaphoreType.DMA((lanes, 2, chips - 1)),
            pltpu.SemaphoreType.DMA((lanes, 2, chips)),
            pltpu.SemaphoreType.DMA((lanes, 2)),
            pltpu.SemaphoreType.DMA((2, chips)),
            pltpu.SemaphoreType.DMA((2,)),
        ],
        compiler_params=pltpu.CompilerParams(
            collective_id=0, has_side_effects=True, vmem_limit_bytes=60 * 1024 * 1024
        ),
        name="relay",
    )(
        carry_act, carry_act_tan, carry_adj, carry_adj_tan, fresh_act, loss_cot, stash_act,
        stash_act_tan, norm_gain, up_weight, down_weight, up_dir, down_dir,
    )
    deep = band * ticks
    stash_sw = stash_out.reshape(deep, width)
    delta_sw = delta_out.reshape(deep, units)
    adj_flat = jnp.swapaxes(adj_out.reshape(ticks, n_dp, 2 * rows, width), 0, 1).reshape(deep, width)
    width_chunk = lane_chunk(width, 256)
    steps = width // width_chunk
    split_units = units % (128 * steps) == 0
    unit_chunk = units // steps if split_units else units
    unit_index = (lambda i: i) if split_units else (lambda i: 0)
    whole = lambda *shape: pl.BlockSpec(shape, lambda i: (0,) * len(shape))
    rows_shape = jax.ShapeDtypeStruct((1, rows, width), bf16)
    return tuple(
        pl.pallas_call(
            functools.partial(curvature_kernel, split_units),
            grid=(steps,),
            out_shape=(rows_shape,) * 4
            + (
                jax.ShapeDtypeStruct((1, width, units), bf16),
                jax.ShapeDtypeStruct((1, units, width), bf16),
            ),
            in_specs=[
                pl.BlockSpec((deep, width_chunk), lambda i: (0, i)),
                whole(deep, units),
                pl.BlockSpec((deep, unit_chunk), lambda i: (0, unit_index(i))),
                whole(deep, width),
                whole(4, rows, width),
            ],
            out_specs=(whole(1, rows, width),) * 4
            + (
                pl.BlockSpec((1, width_chunk, units), lambda i: (0, i, 0)),
                pl.BlockSpec((1, unit_chunk, width), lambda i: (0, unit_index(i), 0)),
            ),
            name="curvature",
        )(stash_sw, delta_sw, hidden_out, adj_flat, final_out)
    )


def solution(mesh):
    in_specs = (
        P("section", "dp", None),
        P("section", "dp", None),
        P("section", "dp", None),
        P("section", "dp", None),
        P(None, "dp", None),
        P(None, "dp", None),
        P("section", None, "dp", None),
        P("section", None, "dp", None),
        P("section", None),
        P("section", None, "dp"),
        P("section", "dp", None),
        P("section", None, "dp"),
        P("section", "dp", None),
    )
    out_specs = (
        P("section", "dp", None),
        P("section", "dp", None),
        P("section", "dp", None),
        P("section", "dp", None),
        P("section", None, "dp"),
        P("section", "dp", None),
    )
    return jax.shard_map(shards, mesh=mesh, in_specs=in_specs, out_specs=out_specs, check_vma=False)
```

time: 400 us -> 67 us (0.17)
  matrix products: 139 us -> 0 us
  waiting for transfers between devices: 130 us -> 0 us
  blocking collectives: 77.8 us -> 0 us
  Pallas kernels: 0 us -> 63.8 us
  starting transfers between devices: 23.7 us -> 0 us
  between operations: 15.1 us -> 0.65 us
  other arithmetic: 11.1 us -> 0 us
    dot_general x36 -> x0, matrix products: 139 us -> none  [the longest x8 55.4 us: product_first(): lax.dot_general(left, right, (((0,), (0,)), ((), ())), preferred_element_...]
    reduce_scatter x8 -> x0, waiting for transfers between devices: 124 us -> none  [the longest x2 38.6 us: reduce_rows(): lax.psum_scatter(forward_term.astype(jnp.bfloat16), 'dp', scatter_dimensi...]
    all_gather x12 -> x0, blocking collectives: 77.8 us -> none  [the longest x2 22.4 us: gather_rows(): lax.all_gather(stash_rows, 'dp', axis=0, tiled=True)]
    pallas_call x0 -> x2, Pallas kernels: none -> 63.8 us  [the longest x1 54.9 us: shards(): pl.pallas_call(functools.partial(relay_kernel, sections, n_dp, ticks), ou...]
    ppermute x8 -> x0, starting transfers between devices: 23.4 us -> none  [passed_along(): lax.ppermute(value, axis, [(source, source + steps) for source in range(l...]
    ppermute x8 -> x0, waiting for transfers between devices: 5.81 us -> none  [passed_along(): lax.ppermute(value, axis, [(source, source + steps) for source in range(l...]
  transfers between devices with their start and end apart: 16 -> 0, of which waited for: 9 -> 0; matrix products, arithmetic and copies ran while one was open for 21% -> 0% of each run, Pallas kernels for 0% -> 0%
where the time goes in v1:
time: 67 us; the launch traced here: 66.4 us
  Pallas kernels  63.8 us (95%)
  local copies, waits for them, and re-layouts  1.95 us (3%)
    pallas_call x1, Pallas kernels, shards(): pl.pallas_call(functools.partial(relay_kernel, sections, n_dp, ticks), ou...  54.9 us
    pallas_call x1, Pallas kernels, shards(): pl.pallas_call(functools.partial(curvature_kernel, split_units), grid=(st...  8.82 us
    reshape x1, local copies, waits for them, and re-layouts, shards(): adj_out.reshape(ticks, n_dp, 2 * rows, width)  1.95 us

profile of v1, /device:TPU:0, one launch (start us, length us, event | category | flops | bytes accessed | tf_op | source)
XLA Modules:
  0.0 66.4 jit_solution(14716822293054088072)
XLA Ops:
  0.6 54.9 %relay.1 = (bf16[2,2,2,16,2304]{4,3,2,1,0:T(8,128)(2,1)}, bf16[2,2,2,16,2304]{4,3,2,1,0:T(8,128)(2,1)}, bf16[128,1152]{1,0:T(8,128)(2,1)}, bf16[4,2,16,1152]{3,2,1,0:T(8,128)(2,1)}, bf16[4,8,2304]{2,1,0:T(8,128)(2,1)}) custom-call(bf16[1,8,2304]{2,1,0:T(8,128)(2,1)} %carry_act.1, bf16[1,8,2304]{2,1,0:T(8,128)(2,1)} %carry_act_tan.1, ...), custom_call_target="tpu_custom_call" | custom-call | tf_op jit(solution)/shard_map/relay/pallas_call | solution.py:445
  55.6 1.9 %copy.19 = bf16[2,4,16,2304]{3,2,0,1:T(8,128)(2,1)} copy(bf16[2,4,16,2304]{3,2,1,0:T(8,128)(2,1)} %bitcast.7) | data formatting | bytes 1179648 | tf_op jit(solution)/shard_map/reshape | solution.py:499
  57.5 8.8 %curvature.1 = (bf16[1,8,2304]{2,1,0:T(8,128)(2,1)}, bf16[1,8,2304]{2,1,0:T(8,128)(2,1)}, bf16[1,8,2304]{2,1,0:T(8,128)(2,1)}, bf16[1,8,2304]{2,1,0:T(8,128)(2,1...) custom-call(bf16[128,2304]{1,0:T(8,128)(2,1)} %bitcast.8, bf16[128,1152]{1,0:T(8,128)(2,1)} %bitcast.9, ...), custom_call_target="tpu_custom_call" | custom-call | tf_op jit(solution)/shard_map/curvature/pallas_call | solution.py:508

commit v2 on v1

--- a/solution.py
+++ b/solution.py
@@ -51,16 +51,28 @@
     return max(fits) if fits else size
 
 
-def over_chunks(size, chunk, body):
-    if size == chunk:
-        body(pl.ds(0, size))
-        return
+def over_chunks(size, chunk, body, after=None):
+    count = size // chunk
 
     def step(index, carry):
-        body(pl.ds(pl.multiple_of(index * chunk, chunk), chunk))
+        start = index * chunk if count == 1 else pl.multiple_of(index * chunk, chunk)
+        body(pl.ds(start, chunk))
+        if after is not None:
+            after(index)
         return carry
 
-    lax.fori_loop(0, size // chunk, step, 0)
+    if count == 1:
+        step(0, 0)
+    else:
+        lax.fori_loop(0, count, step, 0)
+
+
+def once(index, wanted, work):
+    if isinstance(index, int):
+        if index == wanted:
+            work()
+    else:
+        pl.when(index == wanted)(work)
 
 
 def pair(value, tangent):
@@ -97,6 +109,9 @@
     width = carry_act.shape[2]
     units = up.shape[1]
     band = n_dp * 2 * rows
+    unit_chunk = lane_chunk(units, 384)
+    width_chunk = lane_chunk(width, 768)
+    pieces = width // width_chunk
     section, part = (lax.axis_index("section"), lax.axis_index("dp"))
     chip, core = (part // 2, part % 2)
     other = 1 - core
@@ -149,46 +164,56 @@
             device_id_type=MESH,
         )
 
-    def stash_copies():
+    def stash_copies(tick):
         return [
             pltpu.make_async_remote_copy(
-                src_ref=stash_all.at[core, chip],
-                dst_ref=stash_all.at[core, chip],
-                send_sem=stash_sems.at[0, step],
-                recv_sem=stash_sems.at[1, step],
+                src_ref=stash_all.at[tick, core, chip],
+                dst_ref=stash_all.at[tick, core, chip],
+                send_sem=stash_sems.at[tick, 0, step],
+                recv_sem=stash_sems.at[tick, 1, step],
                 device_id=(section, chip_at(step) * 2 + core),
                 device_id_type=MESH,
             )
             for step in range(1, chips)
         ]
 
-    def stash_relay_copy():
+    def stash_relay_copy(tick):
         return pltpu.make_async_remote_copy(
-            src_ref=stash_all.at[core],
-            dst_ref=stash_all.at[core],
-            send_sem=stash_relay.at[0],
-            recv_sem=stash_relay.at[1],
+            src_ref=stash_all.at[tick, core],
+            dst_ref=stash_all.at[tick, core],
+            send_sem=stash_relay.at[tick, 0],
+            recv_sem=stash_relay.at[tick, 1],
             device_id=partner,
             device_id_type=MESH,
         )
 
-    def core_copy(lane):
+    def relay_stash(tick):
+        for copy in stash_copies(tick):
+            copy.wait_recv()
+        stash_relay_copy(tick).start()
+
+    def columns(piece):
+        if isinstance(piece, int):
+            return pl.ds(piece * width_chunk, width_chunk)
+        return pl.ds(pl.multiple_of(piece * width_chunk, width_chunk), width_chunk)
+
+    def core_copy(lane, piece):
         return pltpu.make_async_remote_copy(
-            src_ref=partial.at[lane, other],
-            dst_ref=from_core.at[lane],
-            send_sem=core_sems.at[lane, 0],
-            recv_sem=core_sems.at[lane, 1],
+            src_ref=partial.at[lane, other, :, :, columns(piece)],
+            dst_ref=from_core.at[lane, :, :, columns(piece)],
+            send_sem=core_sems.at[lane, piece, 0],
+            recv_sem=core_sems.at[lane, piece, 1],
             device_id=partner,
             device_id_type=MESH,
         )
 
-    def chip_copies(lane):
+    def chip_copies(lane, piece):
         return [
             pltpu.make_async_remote_copy(
-                src_ref=to_chip.at[lane, step - 1],
-                dst_ref=from_chip.at[lane, step - 1],
-                send_sem=chip_sems.at[lane, 0, step - 1],
-                recv_sem=chip_sems.at[lane, 1, step - 1],
+                src_ref=to_chip.at[lane, step - 1, :, columns(piece)],
+                dst_ref=from_chip.at[lane, step - 1, :, columns(piece)],
+                send_sem=chip_sems.at[lane, piece, 0, step - 1],
+                recv_sem=chip_sems.at[lane, piece, 1, step - 1],
                 device_id=(section, chip_at(step) * 2 + core),
                 device_id_type=MESH,
             )
@@ -214,38 +239,45 @@
             copy.wait_recv()
         relay_copy(lane).start()
 
-    def reduce_in_chip(lane):
-        core_copy(lane).wait_recv()
+    def reduce_in_chip(lane, piece):
+        core_copy(lane, piece).wait_recv()
+        cols = columns(piece)
         for step in range(1, chips):
             place = chip_at(step)
-            summed = partial[lane, core, place].astype(f32) + from_core[lane, place].astype(f32)
-            to_chip[lane, step - 1] = summed.astype(bf16)
-        start_all(chip_copies(lane))
+            summed = partial[lane, core, place, :, cols].astype(f32)
+            summed = summed + from_core[lane, place, :, cols].astype(f32)
+            to_chip[lane, step - 1, :, cols] = summed.astype(bf16)
+        start_all(chip_copies(lane, piece))
 
     def reduced(lane):
+        for piece in range(pieces):
+            for copy in chip_copies(lane, piece):
+                copy.wait_recv()
         total = partial[lane, core, chip].astype(f32) + from_core[lane, chip].astype(f32)
-        for step, copy in enumerate(chip_copies(lane)):
-            copy.wait_recv()
+        for step in range(chips - 1):
             total = total + from_chip[lane, step].astype(f32)
         return (total[:rows], total[rows:])
 
+    def norm_stash(tick):
+        stacked = pair(
+            stash_act[0, tick].astype(f32)[None], stash_act_tan[0, tick].astype(f32)[None]
+        )
+        normed, normed_tan = norm_pair(stacked, gain, rows)
+        stash_all[tick, core, chip] = pair(normed, normed_tan).astype(bf16)
+
     stage_shift(0, carry_act[0].astype(f32), carry_act_tan[0].astype(f32))
+    norm_stash(0)
     pl.semaphore_wait(barrier, 3 * chips)
     start_all(shift_copies(0))
+    start_all(stash_copies(0))
     stage_shift(1, carry_adj[0].astype(f32), carry_adj_tan[0].astype(f32))
+    for tick in range(1, ticks):
+        norm_stash(tick)
+    relay_stash(0)
+    relay(0)
     start_all(shift_copies(1))
-    for tick in range(ticks):
-        stacked = pair(
-            stash_act[0, tick].astype(f32)[None], stash_act_tan[0, tick].astype(f32)[None]
-        )
-        normed, normed_tan = norm_pair(stacked, gain, rows)
-        stash_all[core, chip, tick] = pair(normed, normed_tan).astype(bf16)
-    start_all(stash_copies())
-    relay(0)
-    relay(1)
-    for copy in stash_copies():
-        copy.wait_recv()
-    stash_relay_copy().start()
+    for tick in range(1, ticks):
+        start_all(stash_copies(tick))
 
     outs = []
 
@@ -265,37 +297,33 @@
             left[where, :] = pair(normed, normed_tan).astype(bf16)
             left_dir[where, :] = pair(jnp.zeros_like(normed), normed).astype(bf16)
 
-    stage_forward(0)
-    stash_relay_copy().wait_recv()
-    for block in range(n_dp):
-        for tick in range(ticks):
-            where = pl.ds(band + (block * ticks + tick) * 2 * rows, 2 * rows)
-            stacked = stash_all[block // chips, block % chips, tick]
+    def stage_stash(tick):
+        stash_relay_copy(tick).wait_recv()
+        for block in range(n_dp):
+            where = pl.ds(band + block * 2 * rows, 2 * rows)
+            stacked = stash_all[tick, block // chips, block % chips]
             left[where, :] = stacked
             value = unpair(stacked, rows)[0]
             left_dir[where, :] = pair(jnp.zeros_like(value), value).astype(bf16)
-    send_out(stash_all, stash_out)
-    loads[0].wait()
-    loads[1].wait()
-
-    unit_chunk = lane_chunk(units, 384)
-    width_chunk = lane_chunk(width, 768)
-
-    def up_products(height, with_stash, cols):
-        stacked = matrix_product(left[:height, :], up[:, cols]) + matrix_product(
-            left_dir[:height, :], up_dir[:, cols]
-        )
-        linear, linear_tan = unpair(stacked[:band], rows)
-        value, first, _ = gelu_parts(linear)
-        hid[:, cols] = pair(value, first * linear_tan).astype(bf16)
-        hid_dir[:, cols] = pair(jnp.zeros_like(value), value).astype(bf16)
-        if with_stash:
-            linear, linear_tan = unpair(stacked[band:], rows)
+        send_out(stash_all.at[tick], stash_out.at[tick])
+
+    def up_products(forward, stash_tick, cols):
+        low = 0 if forward else band
+        high = band if stash_tick is None else 2 * band
+        stacked = matrix_product(left[low:high, :], up[:, cols]) + matrix_product(
+            left_dir[low:high, :], up_dir[:, cols]
+        )
+        if forward:
+            linear, linear_tan = unpair(stacked[:band], rows)
+            value, first, _ = gelu_parts(linear)
+            hid[:, cols] = pair(value, first * linear_tan).astype(bf16)
+            hid_dir[:, cols] = pair(jnp.zeros_like(value), value).astype(bf16)
+        if stash_tick is not None:
+            linear, linear_tan = unpair(stacked[band - low :], rows)
             value, first, second = gelu_parts(linear)
-            hid_swap[:, cols] = pair(first * linear_tan, value).astype(bf16)
-            by_tick = (n_dp, ticks, rows, value.shape[-1])
-            slope[:, :, :, cols] = first.reshape(by_tick)
-            bend[:, :, :, cols] = (second * linear_tan).reshape(by_tick)
+            hid_swap[stash_tick, :, cols] = pair(first * linear_tan, value).astype(bf16)
+            slope[stash_tick, :, :, cols] = first
+            bend[stash_tick, :, :, cols] = second * linear_tan
 
     def down_products(lane, cols):
         stacked = matrix_product(hid[...], down[:, cols]) + matrix_product(
@@ -309,14 +337,12 @@
             adj_dir[...], down_dir[cols, :]
         )
         upstream, upstream_tan = unpair(stacked, rows)
-        first, second_tan = (slope[:, tick, :, cols], bend[:, tick, :, cols])
+        first, second_tan = (slope[tick, :, :, cols], bend[tick, :, :, cols])
         value = upstream * first
         tangent = upstream_tan * first + upstream * second_tan
         delta[:, cols] = pair(value, tangent).astype(bf16)
         delta_dir[:, cols] = pair(jnp.zeros_like(value), value).astype(bf16)
-        delta_swap[:, tick, :, cols] = (
-            pair(tangent, value).astype(bf16).reshape(n_dp, 2 * rows, -1)
-        )
+        delta_swap[tick, :, cols] = pair(tangent, value).astype(bf16)
 
     def back_products(lane, cols):
         stacked = product_last(delta[...], up[cols, :]) + product_last(
@@ -366,64 +392,142 @@
             final_out[2] = value.astype(bf16)
             final_out[3] = tangent.astype(bf16)
 
+    def call(work, *given):
+        return functools.partial(work, *given)
+
+    def start_piece(lane, piece):
+        core_copy(lane, piece).start()
+
+    def stage_adjoint(tick):
+        lane = 2 * tick + 1
+        relay_copy(lane).wait_recv()
+        for block in range(n_dp):
+            value = unpair(gathered[lane, block // chips, block % chips], rows)[0]
+            adj_dir[pl.ds(block * 2 * rows, 2 * rows), :] = pair(
+                jnp.zeros_like(value), value
+            ).astype(bf16)
+        send_out(gathered.at[lane], adj_out.at[tick])
+
+    stage_forward(0)
+    stage_stash(0)
+    loads[0].wait()
+    loads[1].wait()
+    last = pieces - 1
     for tick in range(ticks):
         ahead, behind = (2 * tick, 2 * tick + 1)
         if tick:
             stage_forward(tick)
-        height = left.shape[0] if tick == 0 else band
-        over_chunks(units, unit_chunk, functools.partial(up_products, height, tick == 0))
+        over_chunks(units, unit_chunk, call(up_products, True, None if tick else 0))
         if tick == 0:
-            send_out(hid_swap, hidden_out)
+            send_out(hid_swap.at[0], hidden_out.at[0])
             loads[2].wait()
             loads[3].wait()
-        else:
-            relay(behind)
-        over_chunks(width, width_chunk, functools.partial(down_products, ahead))
-        core_copy(ahead).start()
-        relay_copy(behind).wait_recv()
-        for block in range(n_dp):
-            value = unpair(gathered[behind, block // chips, block % chips], rows)[0]
-            adj_dir[pl.ds(block * 2 * rows, 2 * rows), :] = pair(
-                jnp.zeros_like(value), value
-            ).astype(bf16)
-        send_out(gathered.at[behind], adj_out.at[tick])
-        over_chunks(units, unit_chunk, functools.partial(adjoint_products, tick))
-        reduce_in_chip(ahead)
-        over_chunks(width, width_chunk, functools.partial(back_products, behind))
-        core_copy(behind).start()
+        over_chunks(width, width_chunk, call(down_products, ahead), call(start_piece, ahead))
+        relay(behind)
+        stage_adjoint(tick)
+
+        def reduce_pieces(index):
+            def all_pieces():
+                for piece in range(pieces):
+                    reduce_in_chip(ahead, piece)
+
+            once(index, 0, all_pieces)
+
+        over_chunks(units, unit_chunk, call(adjoint_products, tick), reduce_pieces)
+        send_out(delta_swap.at[tick], delta_out.at[tick])
         finish_forward(tick)
-        reduce_in_chip(behind)
         if tick + 1 < ticks:
+            relay_stash(tick + 1)
+
+        def pass_piece(index):
+            start_piece(behind, index)
+            for piece in range(1, pieces):
+                once(index, piece, call(reduce_in_chip, behind, piece - 1))
+
+        over_chunks(width, width_chunk, call(back_products, behind), pass_piece)
+        if tick + 1 < ticks:
+            reduce_in_chip(behind, last)
+            stage_stash(tick + 1)
+            over_chunks(units, unit_chunk, call(up_products, False, tick + 1))
+            send_out(hid_swap.at[tick + 1], hidden_out.at[tick + 1])
             relay(ahead + 2)
         else:
-            send_out(delta_swap, delta_out)
+            reduce_in_chip(behind, last)
         finish_backward(tick)
 
     for lane in range(2 * ticks):
-        for copy in shift_copies(lane) + chip_copies(lane):
+        for copy in shift_copies(lane):
             copy.wait_send()
         relay_copy(lane).wait_send()
-        core_copy(lane).wait_send()
-    for copy in stash_copies():
-        copy.wait_send()
-    stash_relay_copy().wait_send()
+        for piece in range(pieces):
+            core_copy(lane, piece).wait_send()
+            for copy in chip_copies(lane, piece):
+                copy.wait_send()
+    for tick in range(ticks):
+        for copy in stash_copies(tick):
+            copy.wait_send()
+        stash_relay_copy(tick).wait_send()
     for copy in outs:
         copy.wait()
 
 
-def curvature_kernel(split_units, stash_sw, delta_sw, hidden_sw, adj, final, *outs):
-    act, act_tan, adj_new, adj_new_tan, up_out, down_out = outs
-    for index, target in enumerate((act, act_tan, adj_new, adj_new_tan)):
-        target[0] = final[index]
-    up_out[0] = product_first(stash_sw[...], delta_sw[...]).astype(bf16)
-
-    def down():
-        down_out[0] = product_first(hidden_sw[...], adj[...]).astype(bf16)
-
-    if split_units:
-        down()
+def curvature_kernel(
+    stash_hbm, delta_hbm, hidden_hbm, adj_hbm, final_hbm,
+    act, act_tan, adj_new, adj_new_tan, up_hbm, down_hbm,
+    stash_sw, delta_sw, hidden_sw, adj, final, up_out, down_out, in_sems, row_sems, up_sems, down_sems,
+):
+    sources = (stash_hbm, delta_hbm, hidden_hbm, adj_hbm, final_hbm)
+    targets = (stash_sw, delta_sw, hidden_sw, adj, final)
+    loads = [
+        pltpu.make_async_copy(source, target, in_sems.at[i])
+        for i, (source, target) in enumerate(zip(sources, targets))
+    ]
+    for load in loads:
+        load.start()
+    for load in loads:
+        load.wait()
+    row_copies = [
+        pltpu.make_async_copy(final.at[i], target.at[0], row_sems.at[i])
+        for i, target in enumerate((act, act_tan, adj_new, adj_new_tan))
+    ]
+    for copy in row_copies:
+        copy.start()
+
+    def product(left, right, out, target, sems):
+        chunk = out.shape[0] // sems.shape[0]
+
+        def part(piece):
+            where = pl.ds(piece * chunk, chunk)
+            if not isinstance(piece, int):
+                where = pl.ds(pl.multiple_of(piece * chunk, chunk), chunk)
+            out[where, :] = product_first(left[:, where], right[...]).astype(bf16)
+            copy = pltpu.make_async_copy(out.at[where, :], target.at[0, where, :], sems.at[piece])
+            copy.start()
+
+        return part
+
+    up_part = product(stash_sw, delta_sw, up_out, up_hbm, up_sems)
+    down_part = product(hidden_sw, adj, down_out, down_hbm, down_sems)
+    if up_sems.shape[0] == down_sems.shape[0] > 1:
+
+        def step(piece, carry):
+            up_part(piece)
+            down_part(piece)
+            return carry
+
+        lax.fori_loop(0, up_sems.shape[0], step, 0)
     else:
-        pl.when(pl.program_id(0) == 0)(down)
+        for piece in range(up_sems.shape[0]):
+            up_part(piece)
+        for piece in range(down_sems.shape[0]):
+            down_part(piece)
+    for out, target, sems in ((up_out, up_hbm, up_sems), (down_out, down_hbm, down_sems)):
+        chunk = out.shape[0] // sems.shape[0]
+        for piece in range(sems.shape[0]):
+            where = pl.ds(piece * chunk, chunk)
+            pltpu.make_async_copy(out.at[where, :], target.at[0, where, :], sems.at[piece]).wait()
+    for copy in row_copies:
+        copy.wait()
 
 
 def shards(
@@ -435,7 +539,8 @@
     ticks, rows, width = fresh_act.shape
     units = up_weight.shape[2]
     band = n_dp * 2 * rows
-    tall = band * (1 + ticks)
+    tall = 2 * band
+    pieces = width // lane_chunk(width, 768)
     lanes = 2 * ticks
     vmem, anywhere = (
         pl.BlockSpec(memory_space=pltpu.VMEM),
@@ -445,10 +550,10 @@
     stash_out, adj_out, hidden_out, delta_out, final_out = pl.pallas_call(
         functools.partial(relay_kernel, sections, n_dp, ticks),
         out_shape=(
-            jax.ShapeDtypeStruct((2, chips, ticks) + block, bf16),
             jax.ShapeDtypeStruct((ticks, 2, chips) + block, bf16),
-            jax.ShapeDtypeStruct((band * ticks, units), bf16),
-            jax.ShapeDtypeStruct((n_dp, ticks, 2 * rows, units), bf16),
+            jax.ShapeDtypeStruct((ticks, 2, chips) + block, bf16),
+            jax.ShapeDtypeStruct((ticks, band, units), bf16),
+            jax.ShapeDtypeStruct((ticks, band, units), bf16),
             jax.ShapeDtypeStruct((4, rows, width), bf16),
         ),
         in_specs=[vmem] * 9 + [anywhere] * 4,
@@ -462,14 +567,14 @@
             pltpu.VMEM((tall, width), bf16),
             pltpu.VMEM((band, units), bf16),
             pltpu.VMEM((band, units), bf16),
-            pltpu.VMEM((n_dp, ticks, rows, units), f32),
-            pltpu.VMEM((n_dp, ticks, rows, units), f32),
-            pltpu.VMEM((band * ticks, units), bf16),
+            pltpu.VMEM((ticks, n_dp, rows, units), f32),
+            pltpu.VMEM((ticks, n_dp, rows, units), f32),
+            pltpu.VMEM((ticks, band, units), bf16),
             pltpu.VMEM((band, units), bf16),
             pltpu.VMEM((band, units), bf16),
-            pltpu.VMEM((n_dp, ticks, 2 * rows, units), bf16),
+            pltpu.VMEM((ticks, band, units), bf16),
             pltpu.VMEM((band, width), bf16),
-            pltpu.VMEM((2, chips, ticks) + block, bf16),
+            pltpu.VMEM((ticks, 2, chips) + block, bf16),
             pltpu.VMEM((lanes, 2, chips) + block, bf16),
             pltpu.VMEM((lanes,) + block, bf16),
             pltpu.VMEM((lanes, 2, chips) + block, bf16),
@@ -477,13 +582,13 @@
             pltpu.VMEM((lanes, chips - 1) + block, bf16),
             pltpu.VMEM((lanes, chips - 1) + block, bf16),
             pltpu.SemaphoreType.DMA((4,)),
-            pltpu.SemaphoreType.DMA((3 + ticks,)),
-            pltpu.SemaphoreType.DMA((lanes, 2)),
-            pltpu.SemaphoreType.DMA((lanes, 2, chips - 1)),
+            pltpu.SemaphoreType.DMA((4 * ticks,)),
+            pltpu.SemaphoreType.DMA((lanes, pieces, 2)),
+            pltpu.SemaphoreType.DMA((lanes, pieces, 2, chips - 1)),
             pltpu.SemaphoreType.DMA((lanes, 2, chips)),
             pltpu.SemaphoreType.DMA((lanes, 2)),
-            pltpu.SemaphoreType.DMA((2, chips)),
-            pltpu.SemaphoreType.DMA((2,)),
+            pltpu.SemaphoreType.DMA((ticks, 2, chips)),
+            pltpu.SemaphoreType.DMA((ticks, 2)),
         ],
         compiler_params=pltpu.CompilerParams(
             collective_id=0, has_side_effects=True, vmem_limit_bytes=60 * 1024 * 1024
@@ -496,37 +601,35 @@
     deep = band * ticks
     stash_sw = stash_out.reshape(deep, width)
     delta_sw = delta_out.reshape(deep, units)
-    adj_flat = jnp.swapaxes(adj_out.reshape(ticks, n_dp, 2 * rows, width), 0, 1).reshape(deep, width)
-    width_chunk = lane_chunk(width, 256)
-    steps = width // width_chunk
-    split_units = units % (128 * steps) == 0
-    unit_chunk = units // steps if split_units else units
-    unit_index = (lambda i: i) if split_units else (lambda i: 0)
-    whole = lambda *shape: pl.BlockSpec(shape, lambda i: (0,) * len(shape))
+    hidden_sw = hidden_out.reshape(deep, units)
+    adj_flat = adj_out.reshape(deep, width)
     rows_shape = jax.ShapeDtypeStruct((1, rows, width), bf16)
     return tuple(
         pl.pallas_call(
-            functools.partial(curvature_kernel, split_units),
-            grid=(steps,),
+            curvature_kernel,
             out_shape=(rows_shape,) * 4
             + (
                 jax.ShapeDtypeStruct((1, width, units), bf16),
                 jax.ShapeDtypeStruct((1, units, width), bf16),
             ),
-            in_specs=[
-                pl.BlockSpec((deep, width_chunk), lambda i: (0, i)),
-                whole(deep, units),
-                pl.BlockSpec((deep, unit_chunk), lambda i: (0, unit_index(i))),
-                whole(deep, width),
-                whole(4, rows, width),
+            in_specs=[anywhere] * 5,
+            out_specs=(anywhere,) * 6,
+            scratch_shapes=[
+                pltpu.VMEM((deep, width), bf16),
+                pltpu.VMEM((deep, units), bf16),
+                pltpu.VMEM((deep, units), bf16),
+                pltpu.VMEM((deep, width), bf16),
+                pltpu.VMEM((4, rows, width), bf16),
+                pltpu.VMEM((width, units), bf16),
+                pltpu.VMEM((units, width), bf16),
+                pltpu.SemaphoreType.DMA((5,)),
+                pltpu.SemaphoreType.DMA((4,)),
+                pltpu.SemaphoreType.DMA((width // lane_chunk(width, 768),)),
+                pltpu.SemaphoreType.DMA((units // lane_chunk(units, 384),)),
             ],
-            out_specs=(whole(1, rows, width),) * 4
-            + (
-                pl.BlockSpec((1, width_chunk, units), lambda i: (0, i, 0)),
-                pl.BlockSpec((1, unit_chunk, width), lambda i: (0, unit_index(i), 0)),
-            ),
+            compiler_params=pltpu.CompilerParams(vmem_limit_bytes=60 * 1024 * 1024),
             name="curvature",
-        )(stash_sw, delta_sw, hidden_out, adj_flat, final_out)
+        )(stash_sw, delta_sw, hidden_sw, adj_flat, final_out)
     )
 
 

time: 67 us -> 63.1 us (0.942)
  local copies, waits for them, and re-layouts: 1.95 us -> 0 us
  Pallas kernels: 63.8 us -> 62.3 us
    pallas_call x1, Pallas kernels: 8.82 us -> 6.3 us  [shards(): pl.pallas_call(curvature_kernel, out_shape=(rows_shape,) * 4 + (jax.Shape...]
    reshape x1 -> x0, local copies, waits for them, and re-layouts: 1.95 us -> none  [shards(): adj_out.reshape(ticks, n_dp, 2 * rows, width)]
    pallas_call x1, Pallas kernels: 54.9 us -> 56 us  [shards(): pl.pallas_call(functools.partial(relay_kernel, sections, n_dp, ticks), ou...]
where the time goes in v2:
time: 63.1 us; the launch traced here: 62.9 us
  Pallas kernels  62.3 us (99%)
  between operations  0.65 us (1%)
    pallas_call x1, Pallas kernels, shards(): pl.pallas_call(functools.partial(relay_kernel, sections, n_dp, ticks), ou...  56 us
    pallas_call x1, Pallas kernels, shards(): pl.pallas_call(curvature_kernel, out_shape=(rows_shape,) * 4 + (jax.Shape...  6.3 us

profile of v2, /device:TPU:0, one launch (start us, length us, event | category | flops | bytes accessed | tf_op | source)
XLA Modules:
  0.0 62.9 jit_solution(7286620092923565976)
XLA Ops:
  0.6 56.0 %relay.1 = (bf16[2,2,2,16,2304]{4,3,2,1,0:T(8,128)(2,1)}, bf16[2,2,2,16,2304]{4,3,2,1,0:T(8,128)(2,1)}, bf16[2,64,1152]{2,1,0:T(8,128)(2,1)}, bf16[2,64,1152]{2,1,0:T(8,128)(2,1)}, bf16[4,8,2304]{2,1,0:T(8,128)(2,1)}) custom-call(bf16[1,8,2304]{2,1,0:T(8,128)(2,1)} %carry_act.1, bf16[1,8,2304]{2,1,0:T(8,128)(2,1)} %carry_act_tan.1, ...), custom_call_target="tpu_custom_call" | custom-call | tf_op jit(solution)/shard_map/relay/pallas_call | solution.py:550
  56.6 6.3 %curvature.1 = (bf16[1,8,2304]{2,1,0:T(8,128)(2,1)}, bf16[1,8,2304]{2,1,0:T(8,128)(2,1)}, bf16[1,8,2304]{2,1,0:T(8,128)(2,1)}, bf16[1,8,2304]{2,1,0:T(8,128)(2,1...) custom-call(bf16[128,2304]{1,0:T(8,128)(2,1)} %bitcast.4, bf16[128,1152]{1,0:T(8,128)(2,1)} %bitcast.7, ...), custom_call_target="tpu_custom_call" | custom-call | tf_op jit(solution)/shard_map/curvature/pallas_call | solution.py:608
